TPU v7x, 128 devices: a whole 4x4x4 slice. The times are simulated.
128 devices in a mesh: ka: 16 (over x_hi, z, core), band: 8 (over x_lo, y).
Axes of the slice: x: 4 (x_hi: 2, x_lo: 2; x = x_hi * 2 + x_lo), y: 4, z: 4, core: 2. Of those that a mesh axis runs over, the one named last changes fastest.
Arguments:
- occ_rows: bfloat16 [16, 2048, 128], P('ka', 'band'), may hold values from -0.5 to 0.5
- vir_rows: bfloat16 [16, 2048, 896], P('ka', 'band'), may hold values from -0.1875 to 0.1875
- trial_vectors: float32 [16, 2, 128, 896], P('ka', None, None, 'band'), may hold values from -6 to 6
- occ_energy: float32 [16, 128], P('ka'), may hold values from -1.2 to -0.3
- vir_energy: float32 [16, 896], P('ka', 'band'), may hold values from 0.1 to 1.5
- coulomb: bfloat16 [2048, 2048], P('band'), may hold values from -0.0625 to 0.0625
- exch_kernel: bfloat16 [16, 2048, 2048], P(None, 'band'), as said below
- minus_table: int32 [16, 16], replicated, may hold values from 0 to 15, as said below
Outputs:
- sigma_vectors: float32 [16, 2, 128, 896], P('ka', None, None, 'band')
Inputs may be any that keep to these rules, and one draw needn't show every extreme that they name: minus_table[k, q] is the k-point k - q on a group of 16 k-points: every row and every column holds each index once, and one q gives minus_table[k, q] == k for every k. Each exch_kernel[q] is symmetric.
All inputs are finite; a program needn't handle non-finite values.
Results may differ from a plain program's by a relative error of at most 0.0051.
Values may be sent and summed in bfloat16 or wider, within the bound.
A program may use at most 128 MiB of HBM per device.

v0:
```python
import jax
import jax.numpy as jnp
from jax import lax
from jax.sharding import PartitionSpec as P


def sent_to_all(array, axis):
    copies = jnp.broadcast_to(array, (lax.axis_size(axis), *array.shape))
    return lax.all_to_all(copies, axis, split_axis=0, concat_axis=0, tiled=True)


def taken_together(array, axis):
    return sent_to_all(array, axis).sum(axis=0)


def in_order(pieces, dim):
    pieces = jnp.moveaxis(pieces, 0, dim)
    dims = pieces.shape
    return pieces.reshape(*dims[:dim], dims[dim] * dims[dim + 1], *dims[dim + 2 :])


def gather_directly(array, axis, dim):
    pieces = sent_to_all(array, axis)
    return in_order(pieces, dim)


def split_up(array, dim, size):
    before, after = (array.shape[:dim], array.shape[dim + 1 :])
    return jnp.moveaxis(array.reshape(*before, size, -1, *after), dim, 0)


def summed_on_arrival(array, axis, dim):
    size = lax.axis_size(axis)
    pieces = lax.all_to_all(split_up(array, dim, size), axis, 0, 0, tiled=True)
    return jnp.sum(pieces, axis=0)


def per_device(
    occ_rows, vir_rows, trial_vectors, occ_energy, vir_energy, coulomb, exch_kernel, minus_table
):
    vectors = trial_vectors.shape[1]
    own_rows = occ_rows.shape[1]
    kpoints = lax.axis_size("ka")
    self_point = lax.axis_index("ka")
    trial_half = trial_vectors[0].astype(jnp.bfloat16)
    trial_full, vir_full = (
        lax.all_gather(trial_half, "band", axis=2, tiled=True),
        lax.all_gather(vir_rows[0], "band", axis=0, tiled=True),
    )
    auxiliary = vir_full.shape[0]
    occ_own = occ_rows[0]
    vir_own = vir_rows[0]
    mixed_rows = jnp.einsum(
        "ri,via->vra", occ_own, trial_full, preferred_element_type=jnp.float32
    ).astype(jnp.bfloat16)
    pair_block = jnp.einsum(
        "vra,na->vrn", mixed_rows, vir_full, preferred_element_type=jnp.float32
    ).astype(jnp.bfloat16)
    density_own = jnp.sum(
        mixed_rows.astype(jnp.float32) * vir_own.astype(jnp.float32)[None], axis=2
    )
    density_sum = taken_together(density_own, "ka")
    density_half = gather_directly(density_sum.astype(jnp.bfloat16), "band", 1)
    potential = jnp.einsum("vn,rn->vr", density_half, coulomb, preferred_element_type=jnp.float32)
    piece_width = auxiliary // kpoints
    kernel_cols = lax.dynamic_slice_in_dim(exch_kernel, self_point * piece_width, piece_width, 2)
    split_pairs = pair_block.reshape(vectors, own_rows, kpoints, piece_width)
    moved_pairs = jnp.take(
        lax.all_to_all(split_pairs, "ka", split_axis=2, concat_axis=2, tiled=True),
        minus_table,
        axis=2,
    )
    summed = jnp.einsum(
        "vrkqc,qrc->vrkc", moved_pairs, kernel_cols, preferred_element_type=jnp.float32
    )
    screened = lax.all_to_all(
        summed.astype(jnp.bfloat16), "ka", split_axis=2, concat_axis=2, tiled=True
    )
    screened = screened.reshape(vectors, own_rows, auxiliary)
    product = jnp.einsum("vrn,na->vra", screened, vir_full, preferred_element_type=jnp.float32)
    weights = (2.0 * potential[:, :, None] * vir_own.astype(jnp.float32)[None] - product).astype(
        jnp.bfloat16
    )
    partial_sums = jnp.einsum("ri,vra->via", occ_own, weights, preferred_element_type=jnp.float32)
    coupled = summed_on_arrival(partial_sums, "band", 2)
    energy_gaps = vir_energy[0][None, :] - occ_energy[0][:, None]
    return (energy_gaps[None] * trial_vectors[0] + coupled)[None]


def solution(mesh):
    in_specs = (
        P("ka", "band", None),
        P("ka", "band", None),
        P("ka", None, None, "band"),
        P("ka", None),
        P("ka", "band"),
        P("band", None),
        P(None, "band", None),
        P(),
    )
    out_specs = P("ka", None, None, "band")
    return jax.shard_map(
        per_device, mesh=mesh, in_specs=in_specs, out_specs=out_specs, check_vma=False
    )
```

profile of v0, /device:TPU:96, one launch (start us, length us, event | category | flops | bytes accessed | tf_op | source)
XLA Modules:
  0.0 215.4 jit_solution(1257399889311923718)
XLA Ops:
  6.5 0.0 copy-start
  6.5 0.0 copy-start.3
  6.5 0.0 copy-start.4
  6.5 0.0 all-gather.4.cloned.1.call-start
  6.5 0.7 all-gather.4.cloned.1.call-update
  7.3 1.1 bitcast_convert_fusion.1
  8.3 0.3 copy.30
  8.7 0.0 copy-done.3
  8.7 0.0 copy-start.2
  8.7 31.1 %all-gather = bf16[1,2,128,896]{2,3,1,0:T(8,128)(2,1)S(1)} all-gather(bf16[1,2,128,112]{2,3,1,0:T(8,128)(2,1)S(1)} %convert_element_type.33), channel_id=2, replica_groups=mesh['ka'=16,'band'=8] {'band'}, dimensions={3}, use_global_device_ids=true | all-gather | bytes 516096 | tf_op jit(solution)/shard_map/all_gather | solution.py:47
  39.7 0.0 copy-done.4
  39.7 0.4 multiply_reduce_fusion.1
  40.2 0.6 broadcast_in_dim.23
  40.8 6.5 %all-to-all-start = ((f32[16,2,256]{2,1,0:T(2,128)}), f32[16,2,256]{2,1,0:T(2,128)S(1)}, u32[]{:S(2)}, u32[]{:S(2)}) async-start(f32[16,2,256]{2,1,0:T(2,128)} %broadcast_in_dim.23), calls=%async_computation | async-start | bytes 65536 | tf_op jit(solution)/shard_map/all_to_all | solution.py:9
  47.3 13.7 %all-gather.4.cloned.1.call-done = bf16[1,2048,896]{2,1,0:T(8,128)(2,1)} async-done(((bf16[1,256,896]{2,1,0:T(8,128)(2,1)}), bf16[1,2048,896]{2,1,0:T(8,128)(2,1)}) %all-gather.4.cloned.1.call-update) | async-done | bytes 3670032 | tf_op jit(solution)/shard_map/all_gather | solution.py:48
  61.0 4.4 %fusion.7 = bf16[2,32,16,8,128]{4,3,2,1,0:T(8,128)(2,1)S(1)} fusion(bf16[2,256,896]{1,2,0:T(8,128)(2,1)S(1)} %get-tuple-element.6, bf16[1,2048,896]{2,1,0:T(8,128)(2,1)} %all-gather.4.cloned.1.call-done), kind=kOutput, calls=%fused_computation.11 | convolution fusion | flops 1880096768 | bytes 6684672 | tf_op jit(solution)/shard_map/vra,na->vrn/dot_general | solution.py:56
  65.5 0.0 copy-done.2
  65.5 1.9 copy.55
  67.4 0.0 all-to-all-done
  67.4 0.0 copy-start.5
  67.4 6.8 %all-to-all-start.2 = ((bf16[2,256,16,128]{3,1,0,2:T(8,128)(2,1)}), bf16[2,256,16,128]{3,1,0,2:T(8,128)(2,1)S(1)}, u32[]{:S(2)}, u32[]{:S(2)}) async-start(bf16[2,256,16,128]{3,1,0,2:T(8,128)(2,1)} %bitcast.66), calls=%async_computation.2 | async-start | bytes 4194304 | tf_op jit(solution)/shard_map/all_to_all | solution.py:69
  74.2 0.0 copy-done.5
  74.2 0.1 reshape.57
  74.3 2.7 %bitcast_convert_fusion = f32[256,128,16]{1,0,2:T(8,128)} fusion(bf16[16,256,2048]{2,1,0:T(8,128)(2,1)} %param.14, s32[]{:T(128)S(6)} %select_n.12), kind=kLoop, calls=%fused_computation.16 | loop fusion | flops 524288 | bytes 3145732
  77.0 26.1 %all-to-all-done.2 = bf16[2,256,16,128]{3,1,0,2:T(8,128)(2,1)S(1)} async-done(((bf16[2,256,16,128]{3,1,0,2:T(8,128)(2,1)}), bf16[2,256,16,128]{3,1,0,2:T(8,128)(2,1)S(1)}, u32[]{:S(2)}, u32[]{:S(2)}) %all-to-all-start.2) | async-done | bytes 2097184 | tf_op jit(solution)/shard_map/all_to_all | solution.py:69
  103.1 0.6 broadcast_in_dim.24
  103.7 0.7 copy-done.1
  104.4 4.2 %all-to-all-start.1 = ((bf16[8,2,256]{2,1,0:T(2,128)(2,1)}), bf16[8,2,256]{2,1,0:T(2,128)(2,1)S(1)}, u32[]{:S(2)}, u32[]{:S(2)}) async-start(bf16[8,2,256]{2,1,0:T(2,128)(2,1)} %broadcast_in_dim.24), calls=%async_computation.1 | async-start | bytes 16384 | tf_op jit(solution)/shard_map/all_to_all | solution.py:9
  108.6 1.7 copy.34
  110.3 13.9 %gather_fusion = bf16[256,2,256,128]{3,2,1,0:T(8,128)(2,1)} fusion(bf16[2,256,16,128]{3,1,2,0:T(8,128)(2,1)S(1)} %copy.34, s32[1024]{0:T(1024)S(1)} %pad_clamp_fusion), kind=kCustom, calls=%fused_computation | custom fusion | bytes 67109888 | tf_op jit(solution)/shard_map/jit(_take)/gather | solution.py:68
  124.2 17.9 %multiply_reduce_fusion = bf16[256,128,2,16]{1,0,2,3:T(8,128)(2,1)S(1)} fusion(f32[256,128,16]{1,0,2:T(8,128)} %bitcast_convert_fusion, bf16[16,16,2,256,128]{4,3,2,1,0:T(8,128)(2,1)} %bitcast.65, pred[16,16]{1,0:T(8,128)(4,1)S(1)} %compare_and_fusion), kind=kLoop, calls=%fused_computation.1 | loop fusion | flops 66060288 | bytes 37748992
  142.1 2.6 %copy.47 = bf16[256,128,2,16]{0,1,2,3:T(8,128)(2,1)} copy(bf16[256,128,2,16]{1,0,2,3:T(8,128)(2,1)S(1)} %multiply_reduce_fusion) | data formatting | bytes 4194304 | tf_op jit(solution)/shard_map/vrkqc,qrc->vrkc/dot_general | solution.py:73
  144.7 0.0 all-to-all-done.1
  144.7 5.5 %all-to-all-start.3 = ((bf16[2,256,16,128]{1,3,0,2:T(8,128)(2,1)}), bf16[2,256,16,128]{1,3,0,2:T(8,128)(2,1)S(1)}, u32[]{:S(2)}, u32[]{:S(2)}) async-start(bf16[2,256,16,128]{1,3,0,2:T(8,128)(2,1)} %bitcast.67), calls=%async_computation.3 | async-start | bytes 4194304 | tf_op jit(solution)/shard_map/all_to_all | solution.py:76
  150.3 0.0 copy-done
  150.3 0.4 convolution_multiply_fusion
  150.6 28.5 %all-to-all-done.3 = bf16[2,256,16,128]{1,3,0,2:T(8,128)(2,1)S(1)} async-done(((bf16[2,256,16,128]{1,3,0,2:T(8,128)(2,1)}), bf16[2,256,16,128]{1,3,0,2:T(8,128)(2,1)S(1)}, u32[]{:S(2)}, u32[]{:S(2)}) %all-to-all-start.3) | async-done | bytes 2097184 | tf_op jit(solution)/shard_map/all_to_all | solution.py:76
  179.2 1.5 copy.35
  180.7 5.6 %fusion.14 = f32[2,896,128]{2,1,0:T(8,128)S(1)} fusion(bf16[2,256,2048]{1,2,0:T(8,128)(2,1)} %bitcast.68, bf16[1,2048,896]{2,1,0:T(8,128)(2,1)} %all-gather.4.cloned.1.call-done, f32[2,256]{1,0:T(2,128)S(1)} %convolution_multiply_fusion, f32[256,896]{0,1:T(8,128)} %copy-done.2, bf16[1,256,128]{2,1,0:T(8,128)(2,1)S(1)} %copy-done.4), kind=kOutput, calls=%fused_computation.14 | convolution fusion | flops 1997864960 | bytes 7669760 | tf_op jit(solution)/shard_map/ri,vra->via/dot_general | solution.py:84
  186.2 0.0 copy-start.6
  186.2 0.0 copy-start.7
  186.3 1.0 copy.56
  187.2 6.6 %all-to-all-start.4 = ((f32[8,2,128,112]{2,3,1,0:T(8,128)}), f32[8,2,128,112]{2,3,1,0:T(8,128)S(1)}, u32[]{:S(2)}, u32[]{:S(2)}) async-start(f32[8,2,128,112]{2,3,1,0:T(8,128)} %bitcast.64), calls=%async_computation.4 | async-start | bytes 1835008 | tf_op jit(solution)/shard_map/all_to_all | solution.py:34
  193.9 0.0 copy-done.6
  193.9 0.0 copy-done.7
  193.9 0.1 broadcast_subtract_fusion
  194.0 13.9 %all-to-all-done.4 = f32[8,2,128,112]{2,3,1,0:T(8,128)S(1)} async-done(((f32[8,2,128,112]{2,3,1,0:T(8,128)}), f32[8,2,128,112]{2,3,1,0:T(8,128)S(1)}, u32[]{:S(2)}, u32[]{:S(2)}) %all-to-all-start.4) | async-done | bytes 917536 | tf_op jit(solution)/shard_map/all_to_all | solution.py:34
  207.9 0.7 bitcast_add_fusion
  (7 shorter events, 0.1 us)
Async XLA Ops:
  6.5 143.7 %copy-start = (bf16[256,2048]{1,0:T(8,128)(2,1)S(1)}, bf16[256,2048]{1,0:T(8,128)(2,1)}, u32[]{:S(2)}) copy-start(bf16[256,2048]{1,0:T(8,128)(2,1)} %param.13) | copy-start | bytes 3145732
  6.5 2.1 copy-start.3
  6.5 33.2 %copy-start.4 = (bf16[1,256,128]{2,1,0:T(8,128)(2,1)S(1)}, bf16[1,256,128]{2,1,0:T(8,128)(2,1)}, u32[]{:S(2)}) copy-start(bf16[1,256,128]{2,1,0:T(8,128)(2,1)} %param.8) | copy-start | bytes 196612
  6.5 54.5 %all-gather.4.cloned.1.call-start = ((), (), s32[]{:S(2)}) async-start(), calls=%async_computation.5 | async-start | bytes 4128768 | tf_op jit(solution)/shard_map/all_gather | solution.py:48
  8.7 56.8 %copy-start.2 = (f32[256,896]{0,1:T(8,128)}, f32[256,896]{0,1:T(8,128)S(1)}, u32[]{:S(2)}) copy-start(f32[256,896]{0,1:T(8,128)S(1)} %copy.30) | copy-start | bytes 2752516
  40.8 26.6 %all-to-all-start = ((f32[16,2,256]{2,1,0:T(2,128)}), f32[16,2,256]{2,1,0:T(2,128)S(1)}, u32[]{:S(2)}, u32[]{:S(2)}) async-start(f32[16,2,256]{2,1,0:T(2,128)} %broadcast_in_dim.23), calls=%async_computation | async-start | bytes 65536 | tf_op jit(solution)/shard_map/all_to_all | solution.py:9
  67.4 6.8 %copy-start.5 = (s32[16,16]{1,0:T(8,128)S(1)}, s32[16,16]{1,0:T(8,128)}, u32[]{:S(2)}) copy-start(s32[16,16]{1,0:T(8,128)} %param.15) | copy-start | bytes 3076
  67.4 35.7 %all-to-all-start.2 = ((bf16[2,256,16,128]{3,1,0,2:T(8,128)(2,1)}), bf16[2,256,16,128]{3,1,0,2:T(8,128)(2,1)S(1)}, u32[]{:S(2)}, u32[]{:S(2)}) async-start(bf16[2,256,16,128]{3,1,0,2:T(8,128)(2,1)} %bitcast.66), calls=%async_computation.2 | async-start | bytes 4194304 | tf_op jit(solution)/shard_map/all_to_all | solution.py:69
  103.1 1.3 copy-start.1
  104.4 40.3 %all-to-all-start.1 = ((bf16[8,2,256]{2,1,0:T(2,128)(2,1)}), bf16[8,2,256]{2,1,0:T(2,128)(2,1)S(1)}, u32[]{:S(2)}, u32[]{:S(2)}) async-start(bf16[8,2,256]{2,1,0:T(2,128)(2,1)} %broadcast_in_dim.24), calls=%async_computation.1 | async-start | bytes 16384 | tf_op jit(solution)/shard_map/all_to_all | solution.py:9
  144.7 34.5 %all-to-all-start.3 = ((bf16[2,256,16,128]{1,3,0,2:T(8,128)(2,1)}), bf16[2,256,16,128]{1,3,0,2:T(8,128)(2,1)S(1)}, u32[]{:S(2)}, u32[]{:S(2)}) async-start(bf16[2,256,16,128]{1,3,0,2:T(8,128)(2,1)} %bitcast.67), calls=%async_computation.3 | async-start | bytes 4194304 | tf_op jit(solution)/shard_map/all_to_all | solution.py:76
  186.2 7.6 %copy-start.6 = (f32[1,128]{1,0:T(1,128)S(1)}, f32[1,128]{1,0:T(1,128)}, u32[]{:S(2)}) copy-start(f32[1,128]{1,0:T(1,128)} %param.11) | copy-start | bytes 1540
  186.2 7.6 %copy-start.7 = (f32[1,112]{1,0:T(1,128)S(1)}, f32[1,112]{1,0:T(1,128)}, u32[]{:S(2)}) copy-start(f32[1,112]{1,0:T(1,128)} %param.12) | copy-start | bytes 1348
  187.2 20.6 %all-to-all-start.4 = ((f32[8,2,128,112]{2,3,1,0:T(8,128)}), f32[8,2,128,112]{2,3,1,0:T(8,128)S(1)}, u32[]{:S(2)}, u32[]{:S(2)}) async-start(f32[8,2,128,112]{2,3,1,0:T(8,128)} %bitcast.64), calls=%async_computation.4 | async-start | bytes 1835008 | tf_op jit(solution)/shard_map/all_to_all | solution.py:34
Sparse Core Ops, SparseCore 0:
  9.0 52.0 all-gather.3
where the time goes:
time: 216 us; the launch traced here: 215 us
  waiting for transfers between devices  82.9 us (38%)
  blocking collectives  31.1 us (14%)
  starting transfers between devices  29.6 us (14%)
  local copies, waits for them, and re-layouts  25 us (12%)
  other arithmetic  22.5 us (10%)
  between operations  13.5 us (6%)
  matrix products  10.8 us (5%)
    all_gather x1, blocking collectives, per_device(): lax.all_gather(trial_half, 'band', axis=2, tiled=True)  31.1 us
    all_to_all x1, waiting for transfers between devices, per_device(): lax.all_to_all(summed.astype(jnp.bfloat16), 'ka', split_axis=2, concat_ax...  28.5 us
    all_to_all x1, waiting for transfers between devices, per_device(): lax.all_to_all(split_pairs, 'ka', split_axis=2, concat_axis=2, tiled=True)  26.1 us
    unnamed x2, other arithmetic  20.6 us
    gather x1, local copies, waits for them, and re-layouts, per_device(): jnp.take(lax.all_to_all(split_pairs, 'ka', split_axis=2, concat_axis=2, t...  13.9 us
    all_to_all x1, waiting for transfers between devices, summed_on_arrival(): pieces = lax.all_to_all(split_up(array, dim, size), axis, 0, 0, tiled=True)  13.9 us
    all_gather x1, waiting for transfers between devices, per_device(): lax.all_gather(vir_rows[0], 'band', axis=0, tiled=True)  13.7 us
    all_to_all x2, starting transfers between devices, sent_to_all(): return lax.all_to_all(copies, axis, split_axis=0, concat_axis=0, tiled=True)  10.7 us
  transfers between devices with their start and end apart: 6, of which 4 were waited for; matrix products, arithmetic and copies ran while one was open for 22% of the time, Pallas kernels for 0%

commit v1 on v0

--- a/solution.py
+++ b/solution.py
@@ -1,7 +1,24 @@
+import functools
 import jax
 import jax.numpy as jnp
 from jax import lax
 from jax.sharding import PartitionSpec as P
+
+
+def _end_cells(u, group_axis, axis_k, k_dim):
+    taken_in = jnp.concatenate(
+        lax.all_to_all(
+            jnp.stack(jnp.split(u, lax.axis_size(group_axis), axis_k), axis=0),
+            axis_name=group_axis,
+            split_axis=0,
+            concat_axis=0,
+        ),
+        k_dim,
+    )
+    return taken_in
+
+
+remake_results_here = functools.partial(_end_cells, group_axis="ka", axis_k=2, k_dim=2)
 
 
 def sent_to_all(array, axis):
@@ -65,11 +82,7 @@
     piece_width = auxiliary // kpoints
     kernel_cols = lax.dynamic_slice_in_dim(exch_kernel, self_point * piece_width, piece_width, 2)
     split_pairs = pair_block.reshape(vectors, own_rows, kpoints, piece_width)
-    moved_pairs = jnp.take(
-        lax.all_to_all(split_pairs, "ka", split_axis=2, concat_axis=2, tiled=True),
-        minus_table,
-        axis=2,
-    )
+    moved_pairs = jnp.take(remake_results_here(split_pairs), minus_table, axis=2)
     summed = jnp.einsum(
         "vrkqc,qrc->vrkc", moved_pairs, kernel_cols, preferred_element_type=jnp.float32
     )

time: 216 us -> 219 us (1.014)
  local copies, waits for them, and re-layouts: 25 us -> 27.8 us
    split x0 -> x1, local copies, waits for them, and re-layouts: none -> 4.8 us  [_end_cells(): jnp.split(u, lax.axis_size(group_axis), axis_k)]
  transfers between devices with their start and end apart: 6 -> 6, of which waited for: 4 -> 4; matrix products, arithmetic and copies ran while one was open for 22% -> 23% of each run, Pallas kernels for 0% -> 0%
where the time goes in v1:
time: 219 us; the launch traced here: 218 us
  waiting for transfers between devices  82.9 us (38%)
  blocking collectives  31.1 us (14%)
  starting transfers between devices  29.6 us (14%)
  local copies, waits for them, and re-layouts  27.8 us (13%)
  other arithmetic  22.5 us (10%)
  between operations  13.7 us (6%)
  matrix products  10.8 us (5%)
    all_gather x1, blocking collectives, per_device(): lax.all_gather(trial_half, 'band', axis=2, tiled=True)  31.1 us
    all_to_all x1, waiting for transfers between devices, per_device(): lax.all_to_all(summed.astype(jnp.bfloat16), 'ka', split_axis=2, concat_ax...  28.5 us
    all_to_all x1, waiting for transfers between devices, _end_cells(): lax.all_to_all(jnp.stack(jnp.split(u, lax.axis_size(group_axis), axis_k),...  26 us
    unnamed x2, other arithmetic  20.6 us
    gather x1, local copies, waits for them, and re-layouts, per_device(): jnp.take(remake_results_here(split_pairs), minus_table, axis=2)  13.9 us
    all_to_all x1, waiting for transfers between devices, summed_on_arrival(): pieces = lax.all_to_all(split_up(array, dim, size), axis, 0, 0, tiled=True)  13.9 us
    all_gather x1, waiting for transfers between devices, per_device(): lax.all_gather(vir_rows[0], 'band', axis=0, tiled=True)  13.7 us
    all_to_all x2, starting transfers between devices, sent_to_all(): return lax.all_to_all(copies, axis, split_axis=0, concat_axis=0, tiled=True)  10.7 us
  transfers between devices with their start and end apart: 6, of which 4 were waited for; matrix products, arithmetic and copies ran while one was open for 23% of the time, Pallas kernels for 0%

profile of v1, /device:TPU:96, one launch (start us, length us, event | category | flops | bytes accessed | tf_op | source)
XLA Modules:
  0.0 218.3 jit_solution(15779257758847403715)
XLA Ops:
  6.5 0.0 copy-start
  6.5 0.0 copy-start.3
  6.5 0.0 copy-start.4
  6.5 0.0 all-gather.4.cloned.1.call-start
  6.5 0.7 all-gather.4.cloned.1.call-update
  7.3 1.1 bitcast_convert_fusion.1
  8.3 0.3 copy.88
  8.7 0.0 copy-done.3
  8.7 0.0 copy-start.1
  8.7 31.1 %all-gather = bf16[1,2,128,896]{2,3,1,0:T(8,128)(2,1)S(1)} all-gather(bf16[1,2,128,112]{2,3,1,0:T(8,128)(2,1)S(1)} %convert_element_type.33), channel_id=2, replica_groups=mesh['ka'=16,'band'=8] {'band'}, dimensions={3}, use_global_device_ids=true | all-gather | bytes 516096 | tf_op jit(solution)/shard_map/all_gather | solution.py:64
  39.7 0.0 copy-done.4
  39.7 0.4 multiply_reduce_fusion.1
  40.2 0.6 broadcast_in_dim.23
  40.8 6.5 %all-to-all-start = ((f32[16,2,256]{2,1,0:T(2,128)}), f32[16,2,256]{2,1,0:T(2,128)S(1)}, u32[]{:S(2)}, u32[]{:S(2)}) async-start(f32[16,2,256]{2,1,0:T(2,128)} %broadcast_in_dim.23), calls=%async_computation | async-start | bytes 65536 | tf_op jit(solution)/shard_map/all_to_all | solution.py:26
  47.3 13.7 %all-gather.4.cloned.1.call-done = bf16[1,2048,896]{2,1,0:T(8,128)(2,1)} async-done(((bf16[1,256,896]{2,1,0:T(8,128)(2,1)}), bf16[1,2048,896]{2,1,0:T(8,128)(2,1)}) %all-gather.4.cloned.1.call-update) | async-done | bytes 3670032 | tf_op jit(solution)/shard_map/all_gather | solution.py:65
  61.0 4.4 %fusion.4 = bf16[2,256,2048]{2,1,0:T(8,128)(2,1)S(1)} fusion(bf16[2,256,896]{1,2,0:T(8,128)(2,1)S(1)} %get-tuple-element.22, bf16[1,2048,896]{2,1,0:T(8,128)(2,1)} %all-gather.4.cloned.1.call-done), kind=kOutput, calls=%fused_computation.6 | convolution fusion | flops 1880096768 | bytes 6684672 | tf_op jit(solution)/shard_map/vra,na->vrn/dot_general | solution.py:73
  65.5 0.0 copy-done.1
  65.5 0.6 copy.140
  66.1 4.8 %fusion.34 = (bf16[2,256,1,128]{3,2,1,0:T(2,128)(2,1)S(1)}, bf16[2,256,1,128]{3,2,1,0:T(2,128)(2,1)S(1)}, bf16[2,256,1,128]{3,2,1,0:T(2,128)(2,1)S(1)}, bf16[2,2...) fusion(bf16[2,256,16,128]{3,2,1,0:T(8,128)(2,1)S(1)} %bitcast.131), kind=kLoop, calls=%fused_computation.59 | loop fusion | bytes 4194304 | tf_op jit(solution)/shard_map/split | solution.py:11
  71.5 0.0 copy-start.2
  71.5 1.3 copy-done.2
  72.8 0.0 all-to-all-done
  72.8 6.8 %all-to-all-start.2 = ((bf16[16,2,256,1,128]{4,2,1,3,0:T(8,128)(2,1)}), bf16[16,2,256,1,128]{4,2,1,3,0:T(8,128)(2,1)S(1)}, u32[]{:S(2)}, u32[]{:S(2)}) async-start(bf16[16,2,256,1,128]{4,2,1,3,0:T(8,128)(2,1)} %copy-done.2), calls=%async_computation.2 | async-start | bytes 4194304 | tf_op jit(solution)/shard_map/all_to_all | solution.py:10
  79.6 0.0 copy-done.5
  79.6 0.1 reshape.65
  79.7 2.7 %bitcast_convert_fusion = f32[256,128,16]{1,0,2:T(8,128)} fusion(bf16[16,256,2048]{2,1,0:T(8,128)(2,1)} %param.14, s32[]{:T(128)S(6)} %select_n.12), kind=kLoop, calls=%fused_computation.14 | loop fusion | flops 524288 | bytes 3145732
  82.5 26.0 %all-to-all-done.2 = bf16[16,2,256,1,128]{4,2,1,3,0:T(8,128)(2,1)S(1)} async-done(((bf16[16,2,256,1,128]{4,2,1,3,0:T(8,128)(2,1)}), bf16[16,2,256,1,128]{4,2,1,3,0:T(8,128)(2,1)S(1)}, u32[]{:S(2)}, u32[]{:S(2)}) %all-to-all-start.2) | async-done | bytes 2097184 | tf_op jit(solution)/shard_map/all_to_all | solution.py:10
  108.5 0.6 broadcast_in_dim.24
  109.1 4.2 %all-to-all-start.1 = ((bf16[8,2,256]{2,1,0:T(2,128)(2,1)}), bf16[8,2,256]{2,1,0:T(2,128)(2,1)S(1)}, u32[]{:S(2)}, u32[]{:S(2)}) async-start(bf16[8,2,256]{2,1,0:T(2,128)(2,1)} %broadcast_in_dim.24), calls=%async_computation.1 | async-start | bytes 16384 | tf_op jit(solution)/shard_map/all_to_all | solution.py:26
  113.3 13.9 %gather_fusion = bf16[256,2,256,128]{3,2,1,0:T(8,128)(2,1)} fusion(bf16[2,256,16,128]{3,1,0,2:T(8,128)(2,1)S(1)} %bitcast.129, s32[1024]{0:T(1024)S(1)} %pad_clamp_fusion), kind=kCustom, calls=%fused_computation | custom fusion | bytes 67109888 | tf_op jit(solution)/shard_map/jit(_take)/gather | solution.py:85
  127.2 17.9 %multiply_reduce_fusion = bf16[256,128,2,16]{1,0,2,3:T(8,128)(2,1)S(1)} fusion(f32[256,128,16]{1,0,2:T(8,128)} %bitcast_convert_fusion, bf16[16,16,2,256,128]{4,3,2,1,0:T(8,128)(2,1)} %bitcast.130, pred[16,16]{1,0:T(8,128)(4,1)S(1)} %compare_and_fusion), kind=kLoop, calls=%fused_computation.1 | loop fusion | flops 66060288 | bytes 37748992
  145.1 2.6 %copy.119 = bf16[256,128,2,16]{0,1,2,3:T(8,128)(2,1)} copy(bf16[256,128,2,16]{1,0,2,3:T(8,128)(2,1)S(1)} %multiply_reduce_fusion) | data formatting | bytes 4194304 | tf_op jit(solution)/shard_map/vrkqc,qrc->vrkc/dot_general | solution.py:86
  147.7 0.0 all-to-all-done.1
  147.7 5.5 %all-to-all-start.3 = ((bf16[2,256,16,128]{1,3,0,2:T(8,128)(2,1)}), bf16[2,256,16,128]{1,3,0,2:T(8,128)(2,1)S(1)}, u32[]{:S(2)}, u32[]{:S(2)}) async-start(bf16[2,256,16,128]{1,3,0,2:T(8,128)(2,1)} %bitcast.132), calls=%async_computation.3 | async-start | bytes 4194304 | tf_op jit(solution)/shard_map/all_to_all | solution.py:89
  153.2 0.0 copy-done
  153.2 0.4 convolution_multiply_fusion
  153.6 28.5 %all-to-all-done.3 = bf16[2,256,16,128]{1,3,0,2:T(8,128)(2,1)S(1)} async-done(((bf16[2,256,16,128]{1,3,0,2:T(8,128)(2,1)}), bf16[2,256,16,128]{1,3,0,2:T(8,128)(2,1)S(1)}, u32[]{:S(2)}, u32[]{:S(2)}) %all-to-all-start.3) | async-done | bytes 2097184 | tf_op jit(solution)/shard_map/all_to_all | solution.py:89
  182.2 1.5 copy.107
  183.6 5.6 %fusion.11 = f32[2,896,128]{2,1,0:T(8,128)S(1)} fusion(bf16[2,256,2048]{1,2,0:T(8,128)(2,1)} %bitcast.133, bf16[1,2048,896]{2,1,0:T(8,128)(2,1)} %all-gather.4.cloned.1.call-done, f32[2,256]{1,0:T(2,128)S(1)} %convolution_multiply_fusion, f32[256,896]{0,1:T(8,128)} %copy-done.1, bf16[1,256,128]{2,1,0:T(8,128)(2,1)S(1)} %copy-done.4), kind=kOutput, calls=%fused_computation.12 | convolution fusion | flops 1997864960 | bytes 7669760 | tf_op jit(solution)/shard_map/ri,vra->via/dot_general | solution.py:97
  189.2 0.0 copy-start.6
  189.2 0.0 copy-start.7
  189.2 1.0 copy.190
  190.2 6.6 %all-to-all-start.4 = ((f32[8,2,128,112]{2,3,1,0:T(8,128)}), f32[8,2,128,112]{2,3,1,0:T(8,128)S(1)}, u32[]{:S(2)}, u32[]{:S(2)}) async-start(f32[8,2,128,112]{2,3,1,0:T(8,128)} %bitcast.128), calls=%async_computation.4 | async-start | bytes 1835008 | tf_op jit(solution)/shard_map/all_to_all | solution.py:51
  196.8 0.0 copy-done.6
  196.8 0.0 copy-done.7
  196.8 0.1 broadcast_subtract_fusion
  196.9 13.9 %all-to-all-done.4 = f32[8,2,128,112]{2,3,1,0:T(8,128)S(1)} async-done(((f32[8,2,128,112]{2,3,1,0:T(8,128)}), f32[8,2,128,112]{2,3,1,0:T(8,128)S(1)}, u32[]{:S(2)}, u32[]{:S(2)}) %all-to-all-start.4) | async-done | bytes 917536 | tf_op jit(solution)/shard_map/all_to_all | solution.py:51
  210.8 0.7 bitcast_add_fusion
  (23 shorter events, 0.6 us)
Async XLA Ops:
  6.5 146.7 %copy-start = (bf16[256,2048]{1,0:T(8,128)(2,1)S(1)}, bf16[256,2048]{1,0:T(8,128)(2,1)}, u32[]{:S(2)}) copy-start(bf16[256,2048]{1,0:T(8,128)(2,1)} %param.13) | copy-start | bytes 3145732
  6.5 2.1 copy-start.3
  6.5 33.2 %copy-start.4 = (bf16[1,256,128]{2,1,0:T(8,128)(2,1)S(1)}, bf16[1,256,128]{2,1,0:T(8,128)(2,1)}, u32[]{:S(2)}) copy-start(bf16[1,256,128]{2,1,0:T(8,128)(2,1)} %param.8) | copy-start | bytes 196612
  6.5 54.5 %all-gather.4.cloned.1.call-start = ((), (), s32[]{:S(2)}) async-start(), calls=%async_computation.5 | async-start | bytes 4128768 | tf_op jit(solution)/shard_map/all_gather | solution.py:65
  8.7 56.8 %copy-start.1 = (f32[256,896]{0,1:T(8,128)}, f32[256,896]{0,1:T(8,128)S(1)}, u32[]{:S(2)}) copy-start(f32[256,896]{0,1:T(8,128)S(1)} %copy.88) | copy-start | bytes 2752516
  40.8 32.0 %all-to-all-start = ((f32[16,2,256]{2,1,0:T(2,128)}), f32[16,2,256]{2,1,0:T(2,128)S(1)}, u32[]{:S(2)}, u32[]{:S(2)}) async-start(f32[16,2,256]{2,1,0:T(2,128)} %broadcast_in_dim.23), calls=%async_computation | async-start | bytes 65536 | tf_op jit(solution)/shard_map/all_to_all | solution.py:26
  71.5 1.3 copy-start.2
  72.8 6.8 %copy-start.5 = (s32[16,16]{1,0:T(8,128)S(1)}, s32[16,16]{1,0:T(8,128)}, u32[]{:S(2)}) copy-start(s32[16,16]{1,0:T(8,128)} %param.15) | copy-start | bytes 3076
  72.8 35.7 %all-to-all-start.2 = ((bf16[16,2,256,1,128]{4,2,1,3,0:T(8,128)(2,1)}), bf16[16,2,256,1,128]{4,2,1,3,0:T(8,128)(2,1)S(1)}, u32[]{:S(2)}, u32[]{:S(2)}) async-start(bf16[16,2,256,1,128]{4,2,1,3,0:T(8,128)(2,1)} %copy-done.2), calls=%async_computation.2 | async-start | bytes 4194304 | tf_op jit(solution)/shard_map/all_to_all | solution.py:10
  109.1 38.6 %all-to-all-start.1 = ((bf16[8,2,256]{2,1,0:T(2,128)(2,1)}), bf16[8,2,256]{2,1,0:T(2,128)(2,1)S(1)}, u32[]{:S(2)}, u32[]{:S(2)}) async-start(bf16[8,2,256]{2,1,0:T(2,128)(2,1)} %broadcast_in_dim.24), calls=%async_computation.1 | async-start | bytes 16384 | tf_op jit(solution)/shard_map/all_to_all | solution.py:26
  147.7 34.5 %all-to-all-start.3 = ((bf16[2,256,16,128]{1,3,0,2:T(8,128)(2,1)}), bf16[2,256,16,128]{1,3,0,2:T(8,128)(2,1)S(1)}, u32[]{:S(2)}, u32[]{:S(2)}) async-start(bf16[2,256,16,128]{1,3,0,2:T(8,128)(2,1)} %bitcast.132), calls=%async_computation.3 | async-start | bytes 4194304 | tf_op jit(solution)/shard_map/all_to_all | solution.py:89
  189.2 7.6 %copy-start.6 = (f32[1,128]{1,0:T(1,128)S(1)}, f32[1,128]{1,0:T(1,128)}, u32[]{:S(2)}) copy-start(f32[1,128]{1,0:T(1,128)} %param.11) | copy-start | bytes 1540
  189.2 7.6 %copy-start.7 = (f32[1,112]{1,0:T(1,128)S(1)}, f32[1,112]{1,0:T(1,128)}, u32[]{:S(2)}) copy-start(f32[1,112]{1,0:T(1,128)} %param.12) | copy-start | bytes 1348
  190.2 20.6 %all-to-all-start.4 = ((f32[8,2,128,112]{2,3,1,0:T(8,128)}), f32[8,2,128,112]{2,3,1,0:T(8,128)S(1)}, u32[]{:S(2)}, u32[]{:S(2)}) async-start(f32[8,2,128,112]{2,3,1,0:T(8,128)} %bitcast.128), calls=%async_computation.4 | async-start | bytes 1835008 | tf_op jit(solution)/shard_map/all_to_all | solution.py:51
Sparse Core Ops, SparseCore 0:
  9.0 52.0 all-gather.3
